TPU v7x, 32 devices: a whole 2x2x4 slice. The times are simulated.
32 devices in a mesh: dp: 16 (over z, x, core), tensor: 2 (over y).
Axes of the slice: x: 2, y: 2, z: 4, core: 2. Of those that a mesh axis runs over, the one named last changes fastest.
Arguments:
- inputs: bfloat16 [16384, 768], P(('dp', 'tensor')), may hold values from -6 to 6
- lengths: int32 [16], P('dp'), may hold values from 512 to 1024, as said below
- query_weight: bfloat16 [768, 768], P(None, 'tensor'), may hold values from -0.21875 to 0.21875
- query_bias: float32 [768], P('tensor'), may hold values from -3 to 3
- key_weight: bfloat16 [768, 768], P(None, 'tensor'), may hold values from -0.21875 to 0.21875
- value_weight: bfloat16 [768, 768], P(None, 'tensor'), may hold values from -0.21875 to 0.21875
- value_bias: float32 [768], P('tensor'), may hold values from -3 to 3
- proj_weight: bfloat16 [768, 768], P('tensor'), may hold values from -4 to 4
- proj_bias: float32 [768], replicated, may hold values from -3 to 3
- attn_gain: float32 [768], replicated, may hold values from 0.1 to 1.9
- attn_shift: float32 [768], replicated, may hold values from -2 to 2
- up_weight: bfloat16 [768, 3072], P(None, 'tensor'), may hold values from -0.21875 to 0.21875
- up_bias: float32 [3072], P('tensor'), may hold values from -3 to 3
- down_weight: bfloat16 [3072, 768], P('tensor'), may hold values from -0.109375 to 0.109375
- down_bias: float32 [768], replicated, may hold values from -3 to 3
- ffn_gain: float32 [768], replicated, may hold values from 0.1 to 1.9
- ffn_shift: float32 [768], replicated, may hold values from -2 to 2
- filter_couple_scores: float32 [12, 512, 512], P('tensor', 'dp'), may hold values from -5 to 5
- filter_smoothing_jitter: float32 [12, 512, 512], P('tensor', 'dp'), may hold values from -5 to 5
- cotangent: bfloat16 [16384, 768], P(('dp', 'tensor')), may hold values from -6 to 6
Outputs:
- layer_output: bfloat16 [16384, 768], P(('dp', 'tensor'))
- input_grads: bfloat16 [16384, 768], P(('dp', 'tensor'))
- query_grads: float32 [768, 768], P(None, 'tensor')
- key_grads: float32 [768, 768], P(None, 'tensor')
- value_grads: float32 [768, 768], P(None, 'tensor')
- proj_grads: float32 [768, 768], P('tensor')
- up_grads: float32 [768, 3072], P(None, 'tensor')
- down_grads: float32 [3072, 768], P('tensor')
- query_bias_grads: float32 [768], P('tensor')
- value_bias_grads: float32 [768], P('tensor')
- up_bias_grads: float32 [3072], P('tensor')
- proj_bias_grads: float32 [768], replicated
- down_bias_grads: float32 [768], replicated
- attn_gain_grads: float32 [768], replicated
- attn_shift_grads: float32 [768], replicated
- ffn_gain_grads: float32 [768], replicated
- ffn_shift_grads: float32 [768], replicated
- mask_logit_gradients: float32 [12, 512, 512], P('tensor', 'dp')
Inputs may be any that keep to these rules, and one draw needn't show every extreme that they name: Each sequence's live slots are its first lengths[b]; at least one sequence fills all 1024 slots.
All inputs are finite; a program needn't handle non-finite values.
Results may differ from a plain program's by a relative error of at most 0.015.
Values may be sent and summed in bfloat16 or wider, within the bound.
A program may use at most 192 MiB of HBM per device.

v0:
```python
import math
import jax
import jax.numpy as jnp
from jax import lax
from jax.sharding import PartitionSpec as P

HEAD_DIM = 64
softening_heat = 0.5
epsilon = 1e-05


def layer_norm(values, gain, shift):
    centre = values - jnp.mean(values, axis=-1, keepdims=True)
    spread = jnp.mean(centre * centre, axis=-1, keepdims=True)
    inverse = lax.rsqrt(spread + epsilon)
    normal = centre * inverse
    return (normal * gain + shift, normal, inverse)


def norm_back(upstream, normal, inverse, gain):
    scaled = upstream * gain
    first_mean = jnp.mean(scaled, axis=-1, keepdims=True)
    second_mean = jnp.mean(scaled * normal, axis=-1, keepdims=True)
    grad_in = inverse * (scaled - first_mean - normal * second_mean)
    return (grad_in, jnp.sum(upstream * normal, axis=0), jnp.sum(upstream, axis=0))


def on_device(
    inputs,
    lengths,
    query_weight,
    query_bias,
    key_weight,
    value_weight,
    value_bias,
    proj_weight,
    proj_bias,
    attn_gain,
    attn_shift,
    up_weight,
    up_bias,
    down_weight,
    down_bias,
    ffn_gain,
    ffn_shift,
    filter_couple_scores,
    filter_smoothing_jitter,
    cotangent,
):
    rows_half = inputs.shape[0]
    seq_len = rows_half * lax.axis_size("tensor")
    local_width = query_weight.shape[1]
    local_heads = local_width // HEAD_DIM
    window = filter_couple_scores.shape[2]
    blocks = seq_len // window
    score_scale = 1.0 / math.sqrt(HEAD_DIM)
    slot_ids = jnp.arange(seq_len, dtype=jnp.int32)
    live_slots = slot_ids < lengths[0]
    own_live = lax.dynamic_slice_in_dim(live_slots, lax.axis_index("tensor") * rows_half, rows_half)
    softened_filter = jax.nn.sigmoid(
        (filter_couple_scores + filter_smoothing_jitter) / softening_heat
    )
    trainable_focus_filter = lax.all_gather(
        softened_filter.astype(jnp.bfloat16), "dp", axis=1, tiled=True
    )
    full_rows = lax.all_gather(inputs, "tensor", axis=0, tiled=True)
    joint_weight = jnp.concatenate([query_weight, key_weight, value_weight], axis=1)
    joint = jnp.dot(full_rows, joint_weight, preferred_element_type=jnp.float32)
    queries = (joint[:, :local_width] + query_bias).astype(jnp.bfloat16)
    queries = queries.reshape(seq_len, local_heads, HEAD_DIM)
    key_rows = joint[:, local_width : 2 * local_width].astype(jnp.bfloat16)
    key_rows = key_rows.reshape(seq_len, local_heads, HEAD_DIM)
    value_rows = (joint[:, 2 * local_width :] + value_bias).astype(jnp.bfloat16)
    value_rows = value_rows.reshape(seq_len, local_heads, HEAD_DIM)

    def scores_for(query_block):
        scores = (
            jnp.einsum("qhd,khd->hqk", query_block, key_rows, preferred_element_type=jnp.float32)
            * score_scale
        )
        return jnp.where(live_slots[None, None, :], scores, -1e30)

    def apply_mask(softmax_out):
        tiles = (
            softmax_out.reshape(local_heads, window, blocks, window)
            * trainable_focus_filter[:, :, None, :]
        )
        return tiles.reshape(local_heads, window, seq_len)

    def attend(query_block):
        scores = scores_for(query_block)
        row_max = jnp.max(scores, axis=-1)
        exponent = jnp.exp(scores - row_max[..., None])
        row_total = jnp.sum(exponent, axis=-1)
        weighted = apply_mask(exponent / row_total[..., None]).astype(jnp.bfloat16)
        context = jnp.einsum(
            "hqk,khd->qhd", weighted, value_rows, preferred_element_type=jnp.float32
        )
        return (context.astype(jnp.bfloat16), row_max + jnp.log(row_total))

    query_blocks = queries.reshape(blocks, window, local_heads, HEAD_DIM)
    contexts, log_totals = lax.map(attend, query_blocks)
    heads_out = contexts.reshape(seq_len, local_width)
    piece = heads_out
    attn_half = lax.psum_scatter(
        jnp.dot(piece, proj_weight, preferred_element_type=jnp.float32),
        "tensor",
        scatter_dimension=0,
        tiled=True,
    )
    normed, normal_attn, inverse_attn = layer_norm(
        inputs.astype(jnp.float32) + attn_half + proj_bias, attn_gain, attn_shift
    )
    hidden_rows = lax.all_gather(normed.astype(jnp.bfloat16), "tensor", axis=0, tiled=True)
    upper = jnp.dot(hidden_rows, up_weight, preferred_element_type=jnp.float32) + up_bias
    gelu_out, gelu_pull = jax.vjp(lambda given: jax.nn.gelu(given, approximate=False), upper)
    active = gelu_out.astype(jnp.bfloat16)
    piece = active
    ffn_half = lax.psum_scatter(
        jnp.dot(piece, down_weight, preferred_element_type=jnp.float32),
        "tensor",
        scatter_dimension=0,
        tiled=True,
    )
    result, normal_ffn, inverse_ffn = layer_norm(normed + ffn_half + down_bias, ffn_gain, ffn_shift)
    layer_output = result.astype(jnp.bfloat16)
    grad_out = cotangent.astype(jnp.float32) * own_live[:, None].astype(jnp.float32)
    grad_ffn, ffn_gain_grad, ffn_shift_grad = norm_back(grad_out, normal_ffn, inverse_ffn, ffn_gain)
    down_bias_grad = jnp.sum(grad_ffn, axis=0)
    grad_ffn_rows = lax.all_gather(grad_ffn.astype(jnp.bfloat16), "tensor", axis=0, tiled=True)
    down_weight_grad = jnp.einsum(
        "sf,sd->fd", active, grad_ffn_rows, preferred_element_type=jnp.float32
    )
    grad_active = jnp.einsum(
        "sd,fd->sf", grad_ffn_rows, down_weight, preferred_element_type=jnp.float32
    )
    grad_upper = gelu_pull(grad_active)[0].astype(jnp.bfloat16)
    up_bias_grad = jnp.sum(grad_upper, axis=0, dtype=jnp.float32)
    up_weight_grad = jnp.einsum(
        "sd,sf->df", hidden_rows, grad_upper, preferred_element_type=jnp.float32
    )
    piece = grad_upper
    grad_hidden = lax.psum_scatter(
        jnp.einsum("sf,df->sd", piece, up_weight, preferred_element_type=jnp.float32),
        "tensor",
        scatter_dimension=0,
        tiled=True,
    )
    grad_attn, attn_gain_grad, attn_shift_grad = norm_back(
        grad_ffn + grad_hidden, normal_attn, inverse_attn, attn_gain
    )
    proj_bias_grad = jnp.sum(grad_attn, axis=0)
    grad_attn_rows = lax.all_gather(grad_attn.astype(jnp.bfloat16), "tensor", axis=0, tiled=True)
    proj_weight_grad = jnp.einsum(
        "sk,sd->kd", heads_out, grad_attn_rows, preferred_element_type=jnp.float32
    )
    grad_context = jnp.einsum(
        "sd,kd->sk", grad_attn_rows, proj_weight, preferred_element_type=jnp.float32
    ).astype(jnp.bfloat16)

    def attend_back(carry, pieces):
        key_total, value_total, mask_total = carry
        query_block, grad_block, log_block = pieces
        softmax_out = jnp.exp(scores_for(query_block) - log_block[..., None])
        weighted = apply_mask(softmax_out)
        grad_weighted = jnp.einsum(
            "qhd,khd->hqk", grad_block, value_rows, preferred_element_type=jnp.float32
        )
        value_total = value_total + jnp.einsum(
            "hqk,qhd->khd",
            weighted.astype(jnp.bfloat16),
            grad_block,
            preferred_element_type=jnp.float32,
        )
        grad_tiles = grad_weighted.reshape(local_heads, window, blocks, window)
        mask_total = mask_total + jnp.sum(
            grad_tiles * softmax_out.reshape(local_heads, window, blocks, window), axis=2
        )
        grad_softmax = (grad_tiles * trainable_focus_filter[:, :, None, :]).reshape(
            local_heads, window, seq_len
        )
        inner = jnp.sum(grad_weighted * weighted, axis=-1, keepdims=True)
        grad_scores = (softmax_out * (grad_softmax - inner) * score_scale).astype(jnp.bfloat16)
        query_grad = jnp.einsum(
            "hqk,khd->qhd", grad_scores, key_rows, preferred_element_type=jnp.float32
        )
        key_total = key_total + jnp.einsum(
            "hqk,qhd->khd", grad_scores, query_block, preferred_element_type=jnp.float32
        )
        return ((key_total, value_total, mask_total), query_grad.astype(jnp.bfloat16))

    zero_rows = jnp.zeros((seq_len, local_heads, HEAD_DIM), jnp.float32)
    zero_mask = jnp.zeros((local_heads, window, window), jnp.float32)
    (key_total, value_total, mask_total), query_grads = lax.scan(
        attend_back,
        (zero_rows, zero_rows, zero_mask),
        (query_blocks, grad_context.reshape(blocks, window, local_heads, HEAD_DIM), log_totals),
    )
    joint_grad = jnp.concatenate(
        [
            query_grads.reshape(seq_len, local_width),
            key_total.astype(jnp.bfloat16).reshape(seq_len, local_width),
            value_total.astype(jnp.bfloat16).reshape(seq_len, local_width),
        ],
        axis=1,
    )
    joint_weight_grad = jnp.einsum(
        "sd,sk->dk", full_rows, joint_grad, preferred_element_type=jnp.float32
    )
    query_weight_grad = joint_weight_grad[:, :local_width]
    key_weight_grad = joint_weight_grad[:, local_width : 2 * local_width]
    value_weight_grad = joint_weight_grad[:, 2 * local_width :]
    query_bias_grad = jnp.sum(joint_grad[:, :local_width], axis=0, dtype=jnp.float32)
    value_bias_grad = jnp.sum(joint_grad[:, 2 * local_width :], axis=0, dtype=jnp.float32)
    piece = joint_grad
    grad_inputs = lax.psum_scatter(
        jnp.einsum("sk,dk->sd", piece, joint_weight, preferred_element_type=jnp.float32).astype(
            jnp.bfloat16
        ),
        "tensor",
        scatter_dimension=0,
        tiled=True,
    ).astype(jnp.float32)
    input_grads = (grad_attn + grad_inputs).astype(jnp.bfloat16)
    filter_slope_lines = lax.psum_scatter(mask_total, "dp", scatter_dimension=1, tiled=True)
    mask_logit_gradients = (
        filter_slope_lines * softened_filter * (1.0 - softened_filter) / softening_heat
    )
    (
        query_weight_grad,
        key_weight_grad,
        value_weight_grad,
        proj_weight_grad,
        query_bias_grad,
        value_bias_grad,
        up_weight_grad,
        down_weight_grad,
        up_bias_grad,
    ) = lax.psum(
        (
            query_weight_grad,
            key_weight_grad,
            value_weight_grad,
            proj_weight_grad,
            query_bias_grad,
            value_bias_grad,
            up_weight_grad,
            down_weight_grad,
            up_bias_grad,
        ),
        "dp",
    )
    (
        proj_bias_grad,
        down_bias_grad,
        attn_gain_grad,
        attn_shift_grad,
        ffn_gain_grad,
        ffn_shift_grad,
    ) = lax.psum(
        (
            proj_bias_grad,
            down_bias_grad,
            attn_gain_grad,
            attn_shift_grad,
            ffn_gain_grad,
            ffn_shift_grad,
        ),
        ("dp", "tensor"),
    )
    return (
        layer_output,
        input_grads,
        query_weight_grad,
        key_weight_grad,
        value_weight_grad,
        proj_weight_grad,
        up_weight_grad,
        down_weight_grad,
        query_bias_grad,
        value_bias_grad,
        up_bias_grad,
        proj_bias_grad,
        down_bias_grad,
        attn_gain_grad,
        attn_shift_grad,
        ffn_gain_grad,
        ffn_shift_grad,
        mask_logit_gradients,
    )


def solution(mesh):
    in_specs = (
        P(("dp", "tensor"), None),
        P("dp"),
        P(None, "tensor"),
        P("tensor"),
        P(None, "tensor"),
        P(None, "tensor"),
        P("tensor"),
        P("tensor", None),
        P(),
        P(),
        P(),
        P(None, "tensor"),
        P("tensor"),
        P("tensor", None),
        P(),
        P(),
        P(),
        P("tensor", "dp", None),
        P("tensor", "dp", None),
        P(("dp", "tensor"), None),
    )
    out_specs = (
        P(("dp", "tensor"), None),
        P(("dp", "tensor"), None),
        P(None, "tensor"),
        P(None, "tensor"),
        P(None, "tensor"),
        P("tensor", None),
        P(None, "tensor"),
        P("tensor", None),
        P("tensor"),
        P("tensor"),
        P("tensor"),
        P(),
        P(),
        P(),
        P(),
        P(),
        P(),
        P("tensor", "dp", None),
    )
    return jax.shard_map(
        on_device, mesh=mesh, in_specs=in_specs, out_specs=out_specs, check_vma=False
    )
```

profile of v0, /device:TPU:0, one launch (start us, length us, event | category | flops | bytes accessed | tf_op | source)
XLA Modules:
  0.0 1162.9 jit_solution(14874265997577795067)
XLA Ops:
  14.8 24.7 %all-gather.6.cloned.1.call-done = bf16[1024,768]{1,0:T(8,128)(2,1)} async-done(((bf16[512,768]{1,0:T(8,128)(2,1)}), bf16[1024,768]{1,0:T(8,128)(2,1)}) %all-gather.6.cloned.1.call-update) | async-done | bytes 1572880 | tf_op jit(solution)/shard_map/all_gather | solution.py:66
  50.6 37.2 %all-gather.8.cloned.1.call-done = bf16[6,512,512]{2,1,0:T(8,128)(2,1)} async-done(((bf16[6,32,512]{2,1,0:T(8,128)(2,1)}), bf16[6,512,512]{2,1,0:T(8,128)(2,1)}) %all-gather.8.cloned.1.call-update) | async-done | bytes 3145744 | tf_op jit(solution)/shard_map/all_gather | solution.py:63
  88.8 84.2 %while.30 = (s32[]{:T(128)}, bf16[2,512,6,64]{1,3,2,0:T(8,128)(2,1)}, f32[2,6,512]{2,1,0:T(8,128)S(1)}, bf16[2,512,6,64]{1,3,2,0:T(8,128)(2,1)}, bf16[1024,6,64]...) while((s32[]{:T(128)}, ...), condition=%wide.region_3.4_spmd.clone, body=%wide.region_0.3_spmd.clone.sunk | while | flops 846395392 | bytes 103145664 | solution.py:102
  100.1 17.0 %mul.486 = f32[6,512,1024]{2,1,0:T(8,128)} reshape(f32[6,512,2,512]{3,2,1,0:T(2,128)} %mul.485) | data formatting | bytes 25165824 | tf_op jit(solution)/shard_map/while/body/eval_jaxpr/mul | solution.py:85
  142.2 17.0 %mul.486 = f32[6,512,1024]{2,1,0:T(8,128)} reshape(f32[6,512,2,512]{3,2,1,0:T(2,128)} %mul.485) | data formatting | bytes 25165824 | tf_op jit(solution)/shard_map/while/body/eval_jaxpr/mul | solution.py:85
  179.8 41.9 %reduce-scatter.6.cloned.1.call-done = f32[512,768]{1,0:T(8,128)} async-done(((f32[1024,768]{1,0:T(8,128)}), f32[512,768]{1,0:T(8,128)}) %reduce-scatter.6.cloned.1.call-update) | async-done | bytes 1572880 | tf_op jit(solution)/shard_map/reduce_scatter | solution.py:105
  225.9 27.3 %all-gather.10.cloned.1.call-done = bf16[1024,768]{1,0:T(8,128)(2,1)} async-done(((bf16[512,768]{1,0:T(8,128)(2,1)}), bf16[1024,768]{1,0:T(8,128)(2,1)}) %all-gather.10.cloned.1.call-update) | async-done | bytes 1572880 | tf_op jit(solution)/shard_map/all_gather | solution.py:114
  253.2 18.8 %multiply_convert_fusion.9 = (bf16[1024,1536]{1,0:T(8,128)(2,1)S(1)}, f32[1024,1536]{1,0:T(8,128)}, f32[1024,1536]{1,0:T(8,128)}) fusion(f32[1536]{0:T(1024)S(1)} %copy-done.49, bf16[1024,768]{1,0:T(8,128)(2,1)} %all-gather.10.cloned.1.call-done, bf16[768,1536]{1,0:T(8,128)(2,1)S(1)} %copy-done), kind=kOutput, calls=%fused_computation.61 | convolution fusion | flops 2519728128 | bytes 19666944 | tf_op jit(solution)/shard_map/dot_general | solution.py:115
  278.7 42.8 %reduce-scatter.8.cloned.1.call-done = f32[512,768]{1,0:T(8,128)} async-done(((f32[1024,768]{1,0:T(8,128)}), f32[512,768]{1,0:T(8,128)}) %reduce-scatter.8.cloned.1.call-update) | async-done | bytes 1572880 | tf_op jit(solution)/shard_map/reduce_scatter | solution.py:119
  330.2 27.3 %all-gather.12.cloned.1.call-done = bf16[1024,768]{1,0:T(8,128)(2,1)} async-done(((bf16[512,768]{1,0:T(8,128)(2,1)}), bf16[1024,768]{1,0:T(8,128)(2,1)}) %all-gather.12.cloned.1.call-update) | async-done | bytes 1572880 | tf_op jit(solution)/shard_map/all_gather | solution.py:130
  374.4 43.5 %reduce-scatter.10.cloned.1.call-done = f32[512,768]{1,0:T(8,128)} async-done(((f32[1024,768]{1,0:T(8,128)}), f32[512,768]{1,0:T(8,128)}) %reduce-scatter.10.cloned.1.call-update) | async-done | bytes 1572880 | tf_op jit(solution)/shard_map/reduce_scatter | solution.py:143
  425.0 27.3 %all-gather.14.cloned.1.call-done = bf16[1024,768]{1,0:T(8,128)(2,1)} async-done(((bf16[512,768]{1,0:T(8,128)(2,1)}), bf16[1024,768]{1,0:T(8,128)(2,1)}) %all-gather.14.cloned.1.call-update) | async-done | bytes 1572880 | tf_op jit(solution)/shard_map/all_gather | solution.py:153
  464.3 292.9 %while.31 = (s32[]{:T(128)}, f32[1024,6,64]{0,2,1:T(8,128)}, f32[1024,6,64]{0,2,1:T(8,128)S(1)}, f32[6,512,512]{2,1,0:T(8,128)}, bf16[2,512,6,64]{1,3,2,0:T(8,12...) while((s32[]{:T(128)}, f32[1024,6,64]{0,2,1:T(8,128)}, ...), condition=%wide.region_18.19_spmd.clone, body=%wide.region_15.18_spmd.clone.sunk | while | flops 3740476416 | bytes 352058144 | solution.py:194
  494.8 22.4 %reduce_sum.228 = f32[6,512,512]{2,1,0:T(8,128)} reduce(f32[6,512,2,512]{3,2,1,0:T(2,128)} %mul.507, f32[]{:T(128)} %constant.61.clone.11..sunk), dimensions={2}, to_apply=%region_17.17 | reduce | flops 1572864 | bytes 18874372 | tf_op jit(solution)/shard_map/while/body/eval_jaxpr/reduce_sum | solution.py:176
  532.5 17.0 %mul.506 = f32[6,512,1024]{2,1,0:T(8,128)} reshape(f32[6,512,2,512]{3,2,1,0:T(2,128)} %mul.505) | data formatting | bytes 25165824 | tf_op jit(solution)/shard_map/while/body/eval_jaxpr/mul | solution.py:179
  549.5 24.8 %fusion.187 = bf16[2,512,6,64]{1,3,2,0:T(8,128)(2,1)} fusion(bf16[2,512,6,64]{1,3,2,0:T(8,128)(2,1)} %get-tuple-element.530, s32[]{:T(128)S(6)} %copy.74, bf16[1024,6,64]{0,2,1:T(8,128)(2,1)S(1)} %get-tuple-element.547, f32[6,512,1024]{2,1,0:T(8,128)} %mul.506, f32[6,512,1024]{2,1,0:T(8,128)} %copy-done.2, ...), kind=kOutput, calls=%fused_computation.34.clone.1 | convolution fusion | flops 1249054720 | bytes 53906944 | tf_op jit(solution)/shard_map/while/body/eval_jaxpr/hqk,khd->qhd/dot_general | solution.py:184
  584.3 25.5 %bitcast_add_fusion.4 = f32[1024,6,64]{0,2,1:T(8,128)} fusion(f32[1024,6,64]{0,2,1:T(8,128)} %get-tuple-element.527, pred[]{:T(512)S(6)} %compare.3, bf16[2,512,6,64]{1,3,2,0:T(8,128)(2,1)S(1)} %get-tuple-element.546, s32[]{:T(128)S(6)} %copy.74, f32[6,512,1024]{2,1,0:T(8,128)} %mul.506, f32[6,512,1024]{2,1,0:T(8,128)} %copy-done.2, ...), kind=kOutput, calls=%fused_computation.30.clone.1 | convolution fusion | flops 1249644544 | bytes 56266752 | tf_op jit(solution)/shard_map/while/body/eval_jaxpr/hqk,qhd->khd/dot_general | solution.py:187
  640.1 22.4 %reduce_sum.228 = f32[6,512,512]{2,1,0:T(8,128)} reduce(f32[6,512,2,512]{3,2,1,0:T(2,128)} %mul.507, f32[]{:T(128)} %constant.61.clone.11..sunk), dimensions={2}, to_apply=%region_17.17 | reduce | flops 1572864 | bytes 18874372 | tf_op jit(solution)/shard_map/while/body/eval_jaxpr/reduce_sum | solution.py:176
  696.6 24.7 %fusion.187 = bf16[2,512,6,64]{1,3,2,0:T(8,128)(2,1)} fusion(bf16[2,512,6,64]{1,3,2,0:T(8,128)(2,1)} %get-tuple-element.530, s32[]{:T(128)S(6)} %copy.74, bf16[1024,6,64]{0,2,1:T(8,128)(2,1)S(1)} %get-tuple-element.547, f32[6,512,1024]{2,1,0:T(8,128)} %mul.506, f32[6,512,1024]{2,1,0:T(8,128)} %copy-done.2, ...), kind=kOutput, calls=%fused_computation.34.clone.1 | convolution fusion | flops 1249054720 | bytes 53906944 | tf_op jit(solution)/shard_map/while/body/eval_jaxpr/hqk,khd->qhd/dot_general | solution.py:184
  731.3 25.7 %bitcast_add_fusion.4 = f32[1024,6,64]{0,2,1:T(8,128)} fusion(f32[1024,6,64]{0,2,1:T(8,128)} %get-tuple-element.527, pred[]{:T(512)S(6)} %compare.3, bf16[2,512,6,64]{1,3,2,0:T(8,128)(2,1)S(1)} %get-tuple-element.546, s32[]{:T(128)S(6)} %copy.74, f32[6,512,1024]{2,1,0:T(8,128)} %mul.506, f32[6,512,1024]{2,1,0:T(8,128)} %copy-done.2, ...), kind=kOutput, calls=%fused_computation.30.clone.1 | convolution fusion | flops 1249644544 | bytes 56266752 | tf_op jit(solution)/shard_map/while/body/eval_jaxpr/hqk,qhd->khd/dot_general | solution.py:187
  785.2 40.9 %all-reduce = (f32[768]{0:T(1024)}, f32[768]{0:T(1024)}, f32[768]{0:T(1024)}, f32[768]{0:T(1024)}, f32[768]{0:T(1024)}, /*index=5*/f32[768]{0:T(1024)}) all-reduce(f32[768]{0:T(1024)S(1)} %copy-done.36, f32[768]{0:T(1024)S(1)} %copy-done.35, f32[768]{0:T(1024)S(1)} %copy-done.38, ...), channel_id=1, replica_groups=mesh['dp'=16,'tensor'=2] {'dp','tensor'}, use_global_device_ids=true, to_apply=%region_33.34 | all-reduce | flops 4608 | bytes 36864 | tf_op jit(solution)/shard_map/psum | solution.py:260
  826.5 63.8 %all-reduce.1 = (f32[384]{0:T(512)}, f32[384]{0:T(512)}, f32[1536]{0:T(1024)}) all-reduce(f32[384]{0:T(512)S(1)} %reduce_sum.193, f32[384]{0:T(512)S(1)} %reduce_sum.195, f32[1536]{0:T(1024)S(1)} %copy-done.40), channel_id=1, replica_groups=mesh['dp'=16,'tensor'=2] {'dp'}, use_global_device_ids=true, to_apply=%region_27.28 | all-reduce | flops 2304 | bytes 18432 | tf_op jit(solution)/shard_map/psum | solution.py:239
  892.6 163.7 %all-reduce.5.cloned.1.call-done = (f32[768,384]{0,1:T(8,128)}, f32[768,384]{0,1:T(8,128)}, f32[768,384]{0,1:T(8,128)}, f32[384,768]{1,0:T(8,128)}, f32[768,1536]{1,0:T(8,128)}, /*index=5*/f32[1536,768]{1,0:T(8,128)}) async-done(((f32[768,384]{0,1:T(8,128)}, f32[768,384]{0,1:T(8,128)}, f32[768,384]{0,1:T(8,128)}, f32[384,768]{1,0:T(8,128)}, f32[768,1536]{1,0:T(8,128)}, /*index=5*/f32[1536,768]{1,0:T(8,128)}), ...) | async-done | bytes 14155792 | tf_op jit(solution)/shard_map/psum | solution.py:239
  1063.2 82.3 %reduce-scatter.14.cloned.1.call-done = f32[6,32,512]{2,1,0:T(8,128)} async-done(((f32[6,512,512]{2,1,0:T(8,128)}), f32[6,32,512]{2,1,0:T(8,128)}) %reduce-scatter.14.cloned.1.call-update) | async-done | bytes 393232 | tf_op jit(solution)/shard_map/reduce_scatter | solution.py:225
  (239 shorter events, 309.1 us)
Async XLA Ops:
  7.2 246.0 %copy-start = (bf16[768,1536]{1,0:T(8,128)(2,1)S(1)}, bf16[768,1536]{1,0:T(8,128)(2,1)}, u32[]{:S(2)}) copy-start(bf16[768,1536]{1,0:T(8,128)(2,1)} %param.35) | copy-start | bytes 7077892
  7.2 32.3 %all-gather.6.cloned.1.call-start = ((), (), s32[]{:S(2)}) async-start(), calls=%async_computation.5 | async-start | bytes 2359296 | tf_op jit(solution)/shard_map/all_gather | solution.py:66
  8.0 79.9 %all-gather.8.cloned.1.call-start = ((), (), s32[]{:S(2)}) async-start(), calls=%async_computation.6 | async-start | bytes 3342336 | tf_op jit(solution)/shard_map/all_gather | solution.py:63
  10.0 211.6 %reduce-scatter.6.cloned.1.call-start = ((), (), s32[]{:S(2)}) async-start(), calls=%async_computation.7 | async-start | bytes 4718592 | tf_op jit(solution)/shard_map/reduce_scatter | solution.py:105
  174.9 46.7 %copy-start.42 = (f32[768]{0:T(1024)S(1)}, f32[768]{0:T(1024)}, u32[]{:S(2)}) copy-start(f32[768]{0:T(1024)} %param.32) | copy-start | bytes 9220
  179.7 45.0 %copy-start.31 = (f32[768]{0:T(1024)S(1)}, f32[768]{0:T(1024)}, u32[]{:S(2)}) copy-start(f32[768]{0:T(1024)} %param.33) | copy-start | bytes 9220
  179.7 45.0 %copy-start.37 = (f32[768]{0:T(1024)S(1)}, f32[768]{0:T(1024)}, u32[]{:S(2)}) copy-start(f32[768]{0:T(1024)} %param.34) | copy-start | bytes 9220
  179.7 73.5 %copy-start.49 = (f32[1536]{0:T(1024)S(1)}, f32[1536]{0:T(1024)}, u32[]{:S(2)}) copy-start(f32[1536]{0:T(1024)} %param.36) | copy-start | bytes 18436
  179.7 73.5 %all-gather.10.cloned.1.call-start = ((), (), s32[]{:S(2)}) async-start(), calls=%async_computation.8 | async-start | bytes 2359296 | tf_op jit(solution)/shard_map/all_gather | solution.py:114
  225.9 95.6 %reduce-scatter.8.cloned.1.call-start = ((), (), s32[]{:S(2)}) async-start(), calls=%async_computation.9 | async-start | bytes 4718592 | tf_op jit(solution)/shard_map/reduce_scatter | solution.py:119
  273.6 47.9 %copy-start.43 = (f32[768]{0:T(1024)S(1)}, f32[768]{0:T(1024)}, u32[]{:S(2)}) copy-start(f32[768]{0:T(1024)} %param.38) | copy-start | bytes 9220
  277.9 46.5 %copy-start.32 = (f32[768]{0:T(1024)S(1)}, f32[768]{0:T(1024)}, u32[]{:S(2)}) copy-start(f32[768]{0:T(1024)} %param.39) | copy-start | bytes 9220
  277.9 47.9 %copy-start.41 = (f32[768]{0:T(1024)S(1)}, f32[768]{0:T(1024)}, u32[]{:S(2)}) copy-start(f32[768]{0:T(1024)} %param.40) | copy-start | bytes 9220
  277.9 79.6 %all-gather.12.cloned.1.call-start = ((), (), s32[]{:S(2)}) async-start(), calls=%async_computation.10 | async-start | bytes 2359296 | tf_op jit(solution)/shard_map/all_gather | solution.py:130
  330.2 87.7 %reduce-scatter.10.cloned.1.call-start = ((), (), s32[]{:S(2)}) async-start(), calls=%async_computation.11 | async-start | bytes 4718592 | tf_op jit(solution)/shard_map/reduce_scatter | solution.py:143
  374.3 47.4 %copy-start.5 = (f32[512,768]{1,0:T(8,128)S(1)}, f32[512,768]{1,0:T(8,128)}, u32[]{:S(2)}) copy-start(f32[512,768]{1,0:T(8,128)} %copy-done.4) | copy-start | bytes 4718596
  374.3 78.0 %all-gather.14.cloned.1.call-start = ((), (), s32[]{:S(2)}) async-start(), calls=%async_computation.12 | async-start | bytes 2359296 | tf_op jit(solution)/shard_map/all_gather | solution.py:153
  424.9 465.4 %reduce-scatter.12.cloned.1.call-start = ((), (), s32[]{:S(2)}) async-start(), calls=%async_computation.13 | async-start | bytes 2359296 | tf_op jit(solution)/shard_map/reduce_scatter | solution.py:216
  766.4 289.9 %all-reduce.5.cloned.1.call-start = ((), (), s32[]{:S(2)}) async-start(), calls=%async_computation.15 | async-start | bytes 28311552 | tf_op jit(solution)/shard_map/psum | solution.py:239
  784.4 105.9 %copy-start.11 = (f32[512,768]{1,0:T(8,128)S(1)}, f32[512,768]{1,0:T(8,128)}, u32[]{:S(2)}) copy-start(f32[512,768]{1,0:T(8,128)} %copy-done.10) | copy-start | bytes 4718596
  784.4 361.1 %reduce-scatter.14.cloned.1.call-start = ((), (), s32[]{:S(2)}) async-start(), calls=%async_computation.14 | async-start | bytes 6684672 | tf_op jit(solution)/shard_map/reduce_scatter | solution.py:225
  890.4 255.2 %copy-start.22 = (f32[6,32,512]{2,1,0:T(8,128)S(1)}, f32[6,32,512]{2,1,0:T(8,128)}, u32[]{:S(2)}) copy-start(f32[6,32,512]{2,1,0:T(8,128)} %param.41) | copy-start | bytes 1179652
  890.4 255.2 %copy-start.23 = (f32[6,32,512]{2,1,0:T(8,128)S(1)}, f32[6,32,512]{2,1,0:T(8,128)}, u32[]{:S(2)}) copy-start(f32[6,32,512]{2,1,0:T(8,128)} %param.42) | copy-start | bytes 1179652
  1056.3 91.1 %copy-start.24 = (f32[384,768]{1,0:T(8,128)S(1)}, f32[384,768]{1,0:T(8,128)}, u32[]{:S(2)}) copy-start(f32[384,768]{1,0:T(8,128)} %get-tuple-element.561) | copy-start | bytes 3538948
  (47 other events, 350.6 us)
Sparse Core Ops, SparseCore 0:
  9.6 29.8 all-gather.5
  42.3 45.4 all-gather.7
  179.8 41.7 reduce-scatter.5
  226.0 27.1 all-gather.9
  278.0 43.3 reduce-scatter.7
  330.3 27.1 all-gather.11
  374.4 43.4 reduce-scatter.9
  425.0 27.1 all-gather.13
  766.5 26.1 reduce-scatter.11
  798.3 258.0 all-reduce.4
  1060.3 85.1 reduce-scatter.13
where the time goes:
time: 1170 us; the launch traced here: 1160 us
  waiting for transfers between devices  519 us (44%)
  matrix products  227 us (19%)
  local copies, waits for them, and re-layouts  200 us (17%)
  blocking collectives  105 us (9%)
  other arithmetic  95.9 us (8%)
  between operations  15.2 us (1%)
    psum x1, waiting for transfers between devices, on_device(): lax.psum((query_weight_grad, key_weight_grad, value_weight_grad, proj_wei...  164 us
    reduce_scatter x1, waiting for transfers between devices, on_device(): lax.psum_scatter(mask_total, 'dp', scatter_dimension=1, tiled=True)  82.3 us
    psum x1, blocking collectives, on_device(): lax.psum((query_weight_grad, key_weight_grad, value_weight_grad, proj_wei...  63.8 us
    mul x4, local copies, waits for them, and re-layouts, apply_mask(): softmax_out.reshape(local_heads, window, blocks, window)  55.4 us
    dot_general x2, matrix products, attend_back(): jnp.einsum('hqk,qhd->khd', grad_scores, query_block, preferred_element_ty...  51.1 us
    mul x4, local copies, waits for them, and re-layouts, attend_back(): grad_tiles * trainable_focus_filter[:, :, None, :]  50.1 us
    dot_general x2, matrix products, attend_back(): jnp.einsum('hqk,khd->qhd', grad_scores, key_rows, preferred_element_type=...  49.5 us
    reduce_sum x2, other arithmetic, attend_back(): jnp.sum(grad_tiles * softmax_out.reshape(local_heads, window, blocks, win...  44.8 us
  transfers between devices with their start and end apart: 11, of which 10 were waited for; matrix products, arithmetic and copies ran while one was open for 4% of the time, Pallas kernels for 0%

commit v1 on v0

--- a/solution.py
+++ b/solution.py
@@ -7,6 +7,24 @@
 HEAD_DIM = 64
 softening_heat = 0.5
 epsilon = 1e-05
+
+
+def in_order(blocks, dim):
+    blocks = jnp.moveaxis(blocks, 0, dim)
+    lengths = blocks.shape
+    return blocks.reshape(*lengths[:dim], lengths[dim] * lengths[dim + 1], *lengths[dim + 2 :])
+
+
+def collected_by_bits(array, axis):
+    peers = lax.axis_size(axis)
+    parts = array[None]
+    for level in range(peers.bit_length() - 1):
+        bit = 1 << level
+        received = lax.ppermute(parts, axis, [(i, i ^ bit) for i in range(peers)])
+        both = jnp.stack([parts, received])
+        upper = lax.axis_index(axis) >> level & 1
+        parts = jnp.where(upper == 0, both, both[::-1]).reshape(-1, *array.shape)
+    return parts
 
 
 def layer_norm(values, gain, shift):
@@ -63,7 +81,7 @@
     trainable_focus_filter = lax.all_gather(
         softened_filter.astype(jnp.bfloat16), "dp", axis=1, tiled=True
     )
-    full_rows = lax.all_gather(inputs, "tensor", axis=0, tiled=True)
+    full_rows = in_order(collected_by_bits(inputs, "tensor"), 0)
     joint_weight = jnp.concatenate([query_weight, key_weight, value_weight], axis=1)
     joint = jnp.dot(full_rows, joint_weight, preferred_element_type=jnp.float32)
     queries = (joint[:, :local_width] + query_bias).astype(jnp.bfloat16)

time: 1170 us -> 1140 us (0.974)
  waiting for transfers between devices: 519 us -> 488 us
    psum x1, waiting for transfers between devices: 164 us -> 251 us  [on_device(): lax.psum((query_weight_grad, key_weight_grad, value_weight_grad, proj_wei...]
    reduce_scatter x1, waiting for transfers between devices: 82.3 us -> 0.01 us  [on_device(): lax.psum_scatter(mask_total, 'dp', scatter_dimension=1, tiled=True)]
    all_gather x1, waiting for transfers between devices: 37.2 us -> 12.1 us  [on_device(): lax.all_gather(softened_filter.astype(jnp.bfloat16), 'dp', axis=1, tiled=...]
    all_gather x1 -> x0, waiting for transfers between devices: 24.7 us -> none  [on_device(): full_rows = lax.all_gather(inputs, 'tensor', axis=0, tiled=True)]
    ppermute x0 -> x1, waiting for transfers between devices: none -> 14.4 us  [collected_by_bits(): received = lax.ppermute(parts, axis, [(i, i ^ bit) for i in range(peers)])]
    unnamed x104 -> x112, local copies, waits for them, and re-layouts: 31.7 us -> 28.2 us
  transfers between devices with their start and end apart: 11 -> 11, of which waited for: 10 -> 9; matrix products, arithmetic and copies ran while one was open for 4% -> 4% of each run, Pallas kernels for 0% -> 0%
where the time goes in v1:
time: 1140 us; the launch traced here: 1130 us
  waiting for transfers between devices  488 us (43%)
  matrix products  224 us (20%)
  local copies, waits for them, and re-layouts  202 us (18%)
  blocking collectives  102 us (9%)
  other arithmetic  97.5 us (9%)
  between operations  15.5 us (1%)
    psum x1, waiting for transfers between devices, on_device(): lax.psum((query_weight_grad, key_weight_grad, value_weight_grad, proj_wei...  251 us
    psum x1, blocking collectives, on_device(): lax.psum((query_weight_grad, key_weight_grad, value_weight_grad, proj_wei...  62.5 us
    mul x4, local copies, waits for them, and re-layouts, apply_mask(): softmax_out.reshape(local_heads, window, blocks, window)  55.4 us
    dot_general x2, matrix products, attend_back(): jnp.einsum('hqk,qhd->khd', grad_scores, query_block, preferred_element_ty...  50.6 us
    mul x4, local copies, waits for them, and re-layouts, attend_back(): grad_tiles * trainable_focus_filter[:, :, None, :]  50.1 us
    dot_general x2, matrix products, attend_back(): jnp.einsum('hqk,khd->qhd', grad_scores, key_rows, preferred_element_type=...  48.4 us
    reduce_sum x2, other arithmetic, attend_back(): jnp.sum(grad_tiles * softmax_out.reshape(local_heads, window, blocks, win...  44.8 us
    reduce_scatter x1, waiting for transfers between devices, on_device(): lax.psum_scatter(jnp.einsum('sf,df->sd', piece, up_weight, preferred_elem...  43.5 us
  transfers between devices with their start and end apart: 11, of which 9 were waited for; matrix products, arithmetic and copies ran while one was open for 4% of the time, Pallas kernels for 0%

profile of v1, /device:TPU:0, one launch (start us, length us, event | category | flops | bytes accessed | tf_op | source)
XLA Modules:
  0.0 1133.8 jit_solution(2999398556807573448)
XLA Ops:
  59.8 84.2 %while.30 = (s32[]{:T(128)}, bf16[2,512,6,64]{1,3,2,0:T(8,128)(2,1)}, f32[2,6,512]{2,1,0:T(8,128)S(1)}, bf16[2,512,6,64]{1,3,2,0:T(8,128)(2,1)}, bf16[1024,6,64]...) while((s32[]{:T(128)}, ...), condition=%wide.region_3.4_spmd.clone, body=%wide.region_0.3_spmd.clone.sunk | while | flops 846395392 | bytes 103145664 | solution.py:120
  71.2 17.0 %mul.486 = f32[6,512,1024]{2,1,0:T(8,128)} reshape(f32[6,512,2,512]{3,2,1,0:T(2,128)} %mul.485) | data formatting | bytes 25165824 | tf_op jit(solution)/shard_map/while/body/eval_jaxpr/mul | solution.py:103
  113.3 17.0 %mul.486 = f32[6,512,1024]{2,1,0:T(8,128)} reshape(f32[6,512,2,512]{3,2,1,0:T(2,128)} %mul.485) | data formatting | bytes 25165824 | tf_op jit(solution)/shard_map/while/body/eval_jaxpr/mul | solution.py:103
  150.9 41.9 %reduce-scatter.6.cloned.1.call-done = f32[512,768]{1,0:T(8,128)} async-done(((f32[1024,768]{1,0:T(8,128)}), f32[512,768]{1,0:T(8,128)}) %reduce-scatter.6.cloned.1.call-update) | async-done | bytes 1572880 | tf_op jit(solution)/shard_map/reduce_scatter | solution.py:123
  197.0 27.3 %all-gather.7.cloned.1.call-done = bf16[1024,768]{1,0:T(8,128)(2,1)} async-done(((bf16[512,768]{1,0:T(8,128)(2,1)}), bf16[1024,768]{1,0:T(8,128)(2,1)}) %all-gather.7.cloned.1.call-update) | async-done | bytes 1572880 | tf_op jit(solution)/shard_map/all_gather | solution.py:132
  224.3 18.8 %multiply_convert_fusion.9 = (bf16[1024,1536]{1,0:T(8,128)(2,1)S(1)}, f32[1024,1536]{1,0:T(8,128)}, f32[1024,1536]{1,0:T(8,128)}) fusion(f32[1536]{0:T(1024)S(1)} %copy-done.52, bf16[1024,768]{1,0:T(8,128)(2,1)} %all-gather.7.cloned.1.call-done, bf16[768,1536]{1,0:T(8,128)(2,1)S(1)} %copy-done), kind=kOutput, calls=%fused_computation.61 | convolution fusion | flops 2519728128 | bytes 19666944 | tf_op jit(solution)/shard_map/dot_general | solution.py:133
  249.8 42.8 %reduce-scatter.8.cloned.1.call-done = f32[512,768]{1,0:T(8,128)} async-done(((f32[1024,768]{1,0:T(8,128)}), f32[512,768]{1,0:T(8,128)}) %reduce-scatter.8.cloned.1.call-update) | async-done | bytes 1572880 | tf_op jit(solution)/shard_map/reduce_scatter | solution.py:137
  301.3 27.3 %all-gather.9.cloned.1.call-done = bf16[1024,768]{1,0:T(8,128)(2,1)} async-done(((bf16[512,768]{1,0:T(8,128)(2,1)}), bf16[1024,768]{1,0:T(8,128)(2,1)}) %all-gather.9.cloned.1.call-update) | async-done | bytes 1572880 | tf_op jit(solution)/shard_map/all_gather | solution.py:148
  345.5 43.5 %reduce-scatter.10.cloned.1.call-done = f32[512,768]{1,0:T(8,128)} async-done(((f32[1024,768]{1,0:T(8,128)}), f32[512,768]{1,0:T(8,128)}) %reduce-scatter.10.cloned.1.call-update) | async-done | bytes 1572880 | tf_op jit(solution)/shard_map/reduce_scatter | solution.py:161
  396.1 27.3 %all-gather.11.cloned.1.call-done = bf16[1024,768]{1,0:T(8,128)(2,1)} async-done(((bf16[512,768]{1,0:T(8,128)(2,1)}), bf16[1024,768]{1,0:T(8,128)(2,1)}) %all-gather.11.cloned.1.call-update) | async-done | bytes 1572880 | tf_op jit(solution)/shard_map/all_gather | solution.py:171
  435.4 293.5 %while.31 = (s32[]{:T(128)}, f32[1024,6,64]{0,2,1:T(8,128)}, f32[1024,6,64]{0,2,1:T(8,128)S(1)}, f32[6,512,512]{2,1,0:T(8,128)}, bf16[2,512,6,64]{1,3,2,0:T(8,12...) while((s32[]{:T(128)}, f32[1024,6,64]{0,2,1:T(8,128)}, ...), condition=%wide.region_18.19_spmd.clone, body=%wide.region_15.18_spmd.clone.sunk | while | flops 3740476416 | bytes 348912384 | solution.py:212
  450.1 16.9 %mul.507 = f32[6,512,2,512]{3,2,1,0:T(2,128)} reshape(f32[6,512,1024]{2,1,0:T(8,128)} %fusion.188) | data formatting | bytes 25165824 | tf_op jit(solution)/shard_map/while/body/eval_jaxpr/mul | solution.py:195
  467.0 22.4 %reduce_sum.228 = f32[6,512,512]{2,1,0:T(8,128)} reduce(f32[6,512,2,512]{3,2,1,0:T(2,128)} %mul.507, f32[]{:T(128)} %constant.62.clone.11..sunk), dimensions={2}, to_apply=%region_17.17 | reduce | flops 1572864 | bytes 18874372 | tf_op jit(solution)/shard_map/while/body/eval_jaxpr/reduce_sum | solution.py:194
  504.7 17.0 %mul.506 = f32[6,512,1024]{2,1,0:T(8,128)} reshape(f32[6,512,2,512]{3,2,1,0:T(2,128)} %mul.505) | data formatting | bytes 25165824 | tf_op jit(solution)/shard_map/while/body/eval_jaxpr/mul | solution.py:197
  521.7 24.2 %fusion.189 = bf16[2,512,6,64]{1,3,2,0:T(8,128)(2,1)} fusion(bf16[2,512,6,64]{1,3,2,0:T(8,128)(2,1)} %get-tuple-element.494, s32[]{:T(128)S(6)} %copy.75, bf16[1024,6,64]{0,2,1:T(8,128)(2,1)S(1)} %get-tuple-element.511, f32[6,512,1024]{2,1,0:T(8,128)} %mul.506, f32[6,512,1024]{2,1,0:T(8,128)} %copy-done.2, ...), kind=kOutput, calls=%fused_computation.34.clone.1 | convolution fusion | flops 1249054720 | bytes 53906944 | tf_op jit(solution)/shard_map/while/body/eval_jaxpr/hqk,khd->qhd/dot_general | solution.py:202
  555.9 25.1 %bitcast_add_fusion.4 = f32[1024,6,64]{0,2,1:T(8,128)} fusion(f32[1024,6,64]{0,2,1:T(8,128)} %get-tuple-element.491, pred[]{:T(512)S(6)} %compare.3, bf16[2,512,6,64]{1,3,2,0:T(8,128)(2,1)} %get-tuple-element.510, s32[]{:T(128)S(6)} %copy.75, f32[6,512,1024]{2,1,0:T(8,128)} %mul.506, f32[6,512,1024]{2,1,0:T(8,128)} %copy-done.2, ...), kind=kOutput, calls=%fused_computation.30.clone.1 | convolution fusion | flops 1249644544 | bytes 56266752 | tf_op jit(solution)/shard_map/while/body/eval_jaxpr/hqk,qhd->khd/dot_general | solution.py:205
  595.6 16.9 %mul.507 = f32[6,512,2,512]{3,2,1,0:T(2,128)} reshape(f32[6,512,1024]{2,1,0:T(8,128)} %fusion.188) | data formatting | bytes 25165824 | tf_op jit(solution)/shard_map/while/body/eval_jaxpr/mul | solution.py:195
  612.5 22.4 %reduce_sum.228 = f32[6,512,512]{2,1,0:T(8,128)} reduce(f32[6,512,2,512]{3,2,1,0:T(2,128)} %mul.507, f32[]{:T(128)} %constant.62.clone.11..sunk), dimensions={2}, to_apply=%region_17.17 | reduce | flops 1572864 | bytes 18874372 | tf_op jit(solution)/shard_map/while/body/eval_jaxpr/reduce_sum | solution.py:194
  652.0 17.0 %mul.506 = f32[6,512,1024]{2,1,0:T(8,128)} reshape(f32[6,512,2,512]{3,2,1,0:T(2,128)} %mul.505) | data formatting | bytes 25165824 | tf_op jit(solution)/shard_map/while/body/eval_jaxpr/mul | solution.py:197
  669.0 24.2 %fusion.189 = bf16[2,512,6,64]{1,3,2,0:T(8,128)(2,1)} fusion(bf16[2,512,6,64]{1,3,2,0:T(8,128)(2,1)} %get-tuple-element.494, s32[]{:T(128)S(6)} %copy.75, bf16[1024,6,64]{0,2,1:T(8,128)(2,1)S(1)} %get-tuple-element.511, f32[6,512,1024]{2,1,0:T(8,128)} %mul.506, f32[6,512,1024]{2,1,0:T(8,128)} %copy-done.2, ...), kind=kOutput, calls=%fused_computation.34.clone.1 | convolution fusion | flops 1249054720 | bytes 53906944 | tf_op jit(solution)/shard_map/while/body/eval_jaxpr/hqk,khd->qhd/dot_general | solution.py:202
  703.2 25.5 %bitcast_add_fusion.4 = f32[1024,6,64]{0,2,1:T(8,128)} fusion(f32[1024,6,64]{0,2,1:T(8,128)} %get-tuple-element.491, pred[]{:T(512)S(6)} %compare.3, bf16[2,512,6,64]{1,3,2,0:T(8,128)(2,1)} %get-tuple-element.510, s32[]{:T(128)S(6)} %copy.75, f32[6,512,1024]{2,1,0:T(8,128)} %mul.506, f32[6,512,1024]{2,1,0:T(8,128)} %copy-done.2, ...), kind=kOutput, calls=%fused_computation.30.clone.1 | convolution fusion | flops 1249644544 | bytes 56266752 | tf_op jit(solution)/shard_map/while/body/eval_jaxpr/hqk,qhd->khd/dot_general | solution.py:205
  756.2 39.9 %all-reduce = (f32[768]{0:T(1024)}, f32[768]{0:T(1024)}, f32[768]{0:T(1024)}, f32[768]{0:T(1024)}, f32[768]{0:T(1024)}, /*index=5*/f32[768]{0:T(1024)}) all-reduce(f32[768]{0:T(1024)S(1)} %copy-done.40, f32[768]{0:T(1024)S(1)} %copy-done.39, f32[768]{0:T(1024)S(1)} %copy-done.42, ...), channel_id=1, replica_groups=mesh['dp'=16,'tensor'=2] {'dp','tensor'}, use_global_device_ids=true, to_apply=%region_33.34 | all-reduce | flops 4608 | bytes 36864 | tf_op jit(solution)/shard_map/psum | solution.py:278
  796.5 62.5 %all-reduce.1 = (f32[384]{0:T(512)}, f32[384]{0:T(512)}, f32[1536]{0:T(1024)}) all-reduce(f32[384]{0:T(512)S(1)} %reduce_sum.193, f32[384]{0:T(512)S(1)} %reduce_sum.195, f32[1536]{0:T(1024)S(1)} %copy-done.44), channel_id=1, replica_groups=mesh['dp'=16,'tensor'=2] {'dp'}, use_global_device_ids=true, to_apply=%region_27.28 | all-reduce | flops 2304 | bytes 18432 | tf_op jit(solution)/shard_map/psum | solution.py:257
  863.0 250.7 %all-reduce.5.cloned.1.call-done = (f32[768,384]{1,0:T(8,128)}, f32[768,384]{1,0:T(8,128)}, f32[768,384]{1,0:T(8,128)}, f32[384,768]{1,0:T(8,128)}, f32[768,1536]{1,0:T(8,128)}, /*index=5*/f32[1536,768]{1,0:T(8,128)}) async-done(((f32[768,384]{1,0:T(8,128)}, f32[768,384]{1,0:T(8,128)}, f32[768,384]{1,0:T(8,128)}, f32[384,768]{1,0:T(8,128)}, f32[768,1536]{1,0:T(8,128)}, /*index=5*/f32[1536,768]{1,0:T(8,128)}), ...) | async-done | bytes 14155792 | tf_op jit(solution)/shard_map/psum | solution.py:257
  (247 shorter events, 290.1 us)
Async XLA Ops:
  7.2 217.1 %copy-start = (bf16[768,1536]{1,0:T(8,128)(2,1)S(1)}, bf16[768,1536]{1,0:T(8,128)(2,1)}, u32[]{:S(2)}) copy-start(bf16[768,1536]{1,0:T(8,128)(2,1)} %param.35) | copy-start | bytes 7077892
  7.2 51.7 %all-gather.5.cloned.1.call-start = ((), (), s32[]{:S(2)}) async-start(), calls=%async_computation.5 | async-start | bytes 3342336 | tf_op jit(solution)/shard_map/all_gather | solution.py:81
  9.4 183.4 %reduce-scatter.6.cloned.1.call-start = ((), (), s32[]{:S(2)}) async-start(), calls=%async_computation.6 | async-start | bytes 4718592 | tf_op jit(solution)/shard_map/reduce_scatter | solution.py:123
  9.4 20.9 %collective-permute-start = (bf16[1,512,768]{2,1,0:T(8,128)(2,1)}, bf16[1,512,768]{2,1,0:T(8,128)(2,1)}, u32[]{:S(2)}, u32[]{:S(2)}) collective-permute-start(bf16[1,512,768]{2,1,0:T(8,128)(2,1)} %bitcast.158), channel_id=1, source_target_pairs={{0,1},{1,0},{2,3},{3,2},{4,5},{5,4},{6,7},{7,6},{8,9},{9,8},{10,11... | collective-permute-start | bytes 2359304 | tf_op jit(solution)/shard_map/ppermute | solution.py:23
  146.0 46.7 %copy-start.46 = (f32[768]{0:T(1024)S(1)}, f32[768]{0:T(1024)}, u32[]{:S(2)}) copy-start(f32[768]{0:T(1024)} %param.32) | copy-start | bytes 9220
  150.8 45.0 %copy-start.35 = (f32[768]{0:T(1024)S(1)}, f32[768]{0:T(1024)}, u32[]{:S(2)}) copy-start(f32[768]{0:T(1024)} %param.33) | copy-start | bytes 9220
  150.8 45.0 %copy-start.41 = (f32[768]{0:T(1024)S(1)}, f32[768]{0:T(1024)}, u32[]{:S(2)}) copy-start(f32[768]{0:T(1024)} %param.34) | copy-start | bytes 9220
  150.8 73.5 %copy-start.52 = (f32[1536]{0:T(1024)S(1)}, f32[1536]{0:T(1024)}, u32[]{:S(2)}) copy-start(f32[1536]{0:T(1024)} %param.36) | copy-start | bytes 18436
  150.8 73.5 %all-gather.7.cloned.1.call-start = ((), (), s32[]{:S(2)}) async-start(), calls=%async_computation.7 | async-start | bytes 2359296 | tf_op jit(solution)/shard_map/all_gather | solution.py:132
  197.0 95.6 %reduce-scatter.8.cloned.1.call-start = ((), (), s32[]{:S(2)}) async-start(), calls=%async_computation.8 | async-start | bytes 4718592 | tf_op jit(solution)/shard_map/reduce_scatter | solution.py:137
  244.7 47.9 %copy-start.47 = (f32[768]{0:T(1024)S(1)}, f32[768]{0:T(1024)}, u32[]{:S(2)}) copy-start(f32[768]{0:T(1024)} %param.38) | copy-start | bytes 9220
  249.0 46.5 %copy-start.36 = (f32[768]{0:T(1024)S(1)}, f32[768]{0:T(1024)}, u32[]{:S(2)}) copy-start(f32[768]{0:T(1024)} %param.39) | copy-start | bytes 9220
  249.0 47.9 %copy-start.45 = (f32[768]{0:T(1024)S(1)}, f32[768]{0:T(1024)}, u32[]{:S(2)}) copy-start(f32[768]{0:T(1024)} %param.40) | copy-start | bytes 9220
  249.0 79.6 %all-gather.9.cloned.1.call-start = ((), (), s32[]{:S(2)}) async-start(), calls=%async_computation.9 | async-start | bytes 2359296 | tf_op jit(solution)/shard_map/all_gather | solution.py:148
  301.3 87.7 %reduce-scatter.10.cloned.1.call-start = ((), (), s32[]{:S(2)}) async-start(), calls=%async_computation.10 | async-start | bytes 4718592 | tf_op jit(solution)/shard_map/reduce_scatter | solution.py:161
  345.4 47.4 %copy-start.5 = (f32[512,768]{1,0:T(8,128)S(1)}, f32[512,768]{1,0:T(8,128)}, u32[]{:S(2)}) copy-start(f32[512,768]{1,0:T(8,128)} %copy-done.4) | copy-start | bytes 4718596
  345.4 77.9 %all-gather.11.cloned.1.call-start = ((), (), s32[]{:S(2)}) async-start(), calls=%async_computation.11 | async-start | bytes 2359296 | tf_op jit(solution)/shard_map/all_gather | solution.py:171
  396.0 463.0 %reduce-scatter.12.cloned.1.call-start = ((), (), s32[]{:S(2)}) async-start(), calls=%async_computation.12 | async-start | bytes 2359296 | tf_op jit(solution)/shard_map/reduce_scatter | solution.py:234
  736.6 124.6 %reduce-scatter.14.cloned.1.call-start = ((), (), s32[]{:S(2)}) async-start(), calls=%async_computation.13 | async-start | bytes 6684672 | tf_op jit(solution)/shard_map/reduce_scatter | solution.py:243
  737.3 376.5 %all-reduce.5.cloned.1.call-start = ((), (), s32[]{:S(2)}) async-start(), calls=%async_computation.14 | async-start | bytes 28311552 | tf_op jit(solution)/shard_map/psum | solution.py:257
  755.5 41.0 %copy-start.44 = (f32[1536]{0:T(1024)S(1)}, f32[1536]{0:T(1024)}, u32[]{:S(2)}) copy-start(f32[1536]{0:T(1024)} %get-tuple-element.300) | copy-start | bytes 18436
  755.5 103.5 %copy-start.10 = (f32[512,768]{1,0:T(8,128)S(1)}, f32[512,768]{1,0:T(8,128)}, u32[]{:S(2)}) copy-start(f32[512,768]{1,0:T(8,128)} %copy-done.9) | copy-start | bytes 4718596
  755.5 105.6 %copy-start.25 = (f32[6,32,512]{2,1,0:T(8,128)S(1)}, f32[6,32,512]{2,1,0:T(8,128)}, u32[]{:S(2)}) copy-start(f32[6,32,512]{2,1,0:T(8,128)} %param.41) | copy-start | bytes 1179652
  755.5 105.6 %copy-start.26 = (f32[6,32,512]{2,1,0:T(8,128)S(1)}, f32[6,32,512]{2,1,0:T(8,128)}, u32[]{:S(2)}) copy-start(f32[6,32,512]{2,1,0:T(8,128)} %param.42) | copy-start | bytes 1179652
  (49 other events, 291.3 us)
Sparse Core Ops, SparseCore 0:
  10.8 48.0 all-gather.4
  150.9 41.7 reduce-scatter.5
  197.1 27.1 all-gather.6
  249.1 43.3 reduce-scatter.7
  301.4 27.1 all-gather.8
  345.5 43.3 reduce-scatter.9
  396.1 27.1 all-gather.10
  736.7 26.1 reduce-scatter.11
  766.8 85.8 reduce-scatter.13
  858.3 255.4 all-reduce.4
